TPU v7x, 8 devices: a whole 2x2x1 slice. The times are simulated.
8 devices in a mesh: data: 1 (over z), outer: 2 (over y), expert: 4 (over x, core).
Axes of the slice: x: 2, y: 2, z: 1, core: 2. Of those that a mesh axis runs over, the one named last changes fastest.
Arguments:
- x_disp: bfloat16 [8, 40, 32, 1536], P('data', ('outer', 'expert'))
- w_gate: bfloat16 [40, 1536, 512], P(('outer', 'expert'))
- w_up: bfloat16 [40, 1536, 512], P(('outer', 'expert'))
- w_down: bfloat16 [40, 512, 1536], P(('outer', 'expert'))
- slot_idx: int32 [1280, 8], P(('data', 'outer', 'expert'))
- expert_ids: int32 [1280, 8], P(('data', 'outer', 'expert'))
- gate_wts: float32 [1280, 8], P(('data', 'outer', 'expert'))
Outputs:
- output: bfloat16 [1280, 1536], P(('data', 'outer', 'expert'))
All inputs are finite; a program needn't handle non-finite values.
Results may differ from a plain program's by a relative error of at most 0.00823053.
Values are sent between devices in bfloat16 or wider.
A program may use at most 1 GiB of HBM per device.

v0:
```python
import jax
import jax.numpy as jnp
from jax import lax
from jax.sharding import PartitionSpec as P


def expert_rows(x_disp, w_gate, w_up, w_down):
    gate_proj = jnp.einsum("secd,edf->secf", x_disp, w_gate, preferred_element_type=jnp.float32)
    up_proj = jnp.einsum("secd,edf->secf", x_disp, w_up, preferred_element_type=jnp.float32)
    hidden = (jax.nn.silu(gate_proj) * up_proj).astype(jnp.bfloat16)
    return jnp.einsum("secf,efd->secd", hidden, w_down, preferred_element_type=jnp.float32).astype(jnp.bfloat16)


def weighted_sum(y_flat, capacity, slot_idx, expert_ids, gate_wts):
    kept_mask = slot_idx >= 0
    flat_idx = jnp.where(kept_mask, expert_ids * capacity + slot_idx, 0)
    weight = jnp.where(kept_mask, gate_wts, 0.0)
    picked = jnp.take(y_flat, flat_idx, axis=0)
    return jnp.sum(picked.astype(jnp.float32) * weight[:, :, None], axis=1).astype(jnp.bfloat16)


def solution(mesh):
    outer_devs = mesh.shape["outer"]
    inner_devs = mesh.shape["expert"]

    def local_step(x_disp, w_gate, w_up, w_down, slot_idx, expert_ids, gate_wts):
        group_devs, local_experts, capacity, model_width = x_disp.shape
        y_local = expert_rows(x_disp, w_gate, w_up, w_down)
        y_split = y_local.reshape(outer_devs, inner_devs, local_experts, capacity, model_width)
        y_inner = lax.all_to_all(y_split, "expert", 1, 1, tiled=True)
        y_recv = lax.all_to_all(y_inner, "outer", 0, 0, tiled=True)
        y_flat = y_recv.reshape(group_devs * local_experts * capacity, model_width)
        return weighted_sum(y_flat, capacity, slot_idx, expert_ids, gate_wts)

    expert_spec = P(("outer", "expert"))
    token_spec = P(("data", "outer", "expert"))
    return jax.shard_map(local_step, mesh=mesh, in_specs=(P("data", ("outer", "expert")), expert_spec, expert_spec, expert_spec, token_spec, token_spec, token_spec), out_specs=token_spec, check_vma=False)
```

profile of v0, /device:TPU:0, one launch (start us, length us, event | category | flops | bytes accessed | tf_op | source)
XLA Modules:
  0.0 145.5 jit_solution(894345837155003708)
XLA Ops:
  0.0 6.5 %fusion.2 = f32[5,512,8,32]{1,3,2,0:T(8,128)S(1)} fusion(bf16[5,1536,512]{2,1,0:T(8,128)(2,1)} %param.9, bf16[8,5,32,1536]{3,2,1,0:T(8,128)(2,1)} %param.7), kind=kOutput, calls=%fused_computation.3 | convolution fusion | flops 2013265920 | bytes 14417920 | tf_op jit(solution)/shard_map/secd,edf->secf/dot_general | solution.py:9
  6.5 12.9 %fusion.6 = bf16[5,8,32,1536]{3,2,1,0:T(8,128)(2,1)} fusion(bf16[5,512,1536]{2,1,0:T(8,128)(2,1)} %param.10, f32[5,512,8,32]{1,3,2,0:T(8,128)S(1)} %fusion.2, bf16[8,5,32,1536]{3,2,1,0:T(8,128)(2,1)} %param.7, bf16[5,1536,512]{2,1,0:T(8,128)(2,1)} %param.8), kind=kOutput, calls=%fused_computation.8 | convolution fusion | flops 4032430080 | bytes 26214400 | tf_op jit(solution)/shard_map/secf,efd->secd/dot_general | solution.py:11
  19.4 2.5 %copy.20 = bf16[2,4,5,32,1536]{4,3,0,2,1:T(8,128)(2,1)S(1)} copy(bf16[2,4,5,32,1536]{4,3,1,0,2:T(8,128)(2,1)} %bitcast.51) | data formatting | bytes 7864320 | tf_op jit(solution)/shard_map/reshape | solution.py:29
  21.9 49.7 %all_to_all.10 = bf16[2,4,5,32,1536]{4,3,0,2,1:T(8,128)(2,1)S(1)} all-to-all(bf16[2,4,5,32,1536]{4,3,0,2,1:T(8,128)(2,1)S(1)} %copy.20), channel_id=1, replica_groups=mesh['data'=1,'outer'=2,'expert'=4] {'expert'}, dimensions={1} | all-to-all | bytes 7864320 | tf_op jit(solution)/shard_map/all_to_all | solution.py:30
  71.7 2.3 %copy.21 = bf16[2,4,5,32,1536]{4,3,1,2,0:T(8,128)(2,1)} copy(bf16[2,4,5,32,1536]{4,3,0,2,1:T(8,128)(2,1)S(1)} %all_to_all.10) | data formatting | bytes 7864320 | tf_op jit(solution)/shard_map/all_to_all | solution.py:30
  74.0 0.0 copy-start
  74.0 0.0 copy-start.2
  74.0 0.0 copy-start.1
  74.0 5.6 %all-to-all-start.1 = ((bf16[2,4,5,32,1536]{4,3,1,2,0:T(8,128)(2,1)}), bf16[2,4,5,32,1536]{4,3,1,2,0:T(8,128)(2,1)}, u32[]{:S(2)}, u32[]{:S(2)}) async-start(bf16[2,4,5,32,1536]{4,3,1,2,0:T(8,128)(2,1)} %copy.21), calls=%async_computation.1 | async-start | bytes 7864320 | tf_op jit(solution)/shard_map/all_to_all | solution.py:31
  79.7 0.0 copy-done
  79.7 0.0 copy-done.2
  79.7 0.1 copy.23
  79.8 0.1 reshape.16
  79.9 0.0 copy-done.1
  79.9 0.1 copy.24
  80.0 0.1 copy.17
  80.2 43.6 %all-to-all-done.1 = bf16[2,4,5,32,1536]{4,3,1,2,0:T(8,128)(2,1)} async-done(((bf16[2,4,5,32,1536]{4,3,1,2,0:T(8,128)(2,1)}), bf16[2,4,5,32,1536]{4,3,1,2,0:T(8,128)(2,1)}, u32[]{:S(2)}, u32[]{:S(2)}) %all-to-all-start.1) | async-done | bytes 3932192 | tf_op jit(solution)/shard_map/all_to_all | solution.py:31
  123.8 4.5 %copy.22 = bf16[2,4,5,32,1536]{4,3,2,1,0:T(8,128)(2,1)} copy(bf16[2,4,5,32,1536]{4,3,1,2,0:T(8,128)(2,1)} %all-to-all-done.1) | data formatting | bytes 7864320 | tf_op jit(solution)/shard_map/all_to_all | solution.py:31
  128.3 11.5 %gather_fusion = bf16[1280,1536]{1,0:T(8,128)(2,1)} fusion(bf16[1280,1536]{1,0:T(8,128)(2,1)} %bitcast.50, s32[2048]{0:T(1024)S(1)} %pad_clamp_fusion), kind=kCustom, calls=%fused_computation | custom fusion | bytes 7869440 | tf_op jit(solution)/shard_map/jit(_take)/gather | solution.py:18
  139.8 5.7 %multiply_reduce_fusion = bf16[160,1536]{1,0:T(8,128)(2,1)} fusion(bf16[1280,1536]{1,0:T(8,128)(2,1)} %gather_fusion, f32[160,8]{1,0:T(8,128)S(1)} %copy.24, pred[160,8]{1,0:T(8,128)(4,1)S(1)} %copy.17), kind=kLoop, calls=%fused_computation.7 | loop fusion | flops 7618560 | bytes 4430080 | tf_op jit(solution)/shard_map/reduce_sum | solution.py:19
  (3 shorter events, 0.0 us)
Async XLA Ops:
  74.0 5.7 %copy-start = (s32[160,8]{0,1:T(8,128)S(1)}, s32[160,8]{0,1:T(8,128)}, u32[]{:S(2)}) copy-start(s32[160,8]{0,1:T(8,128)} %param.11) | copy-start | bytes 15364
  74.0 5.7 %copy-start.2 = (s32[160,8]{0,1:T(8,128)S(1)}, s32[160,8]{0,1:T(8,128)}, u32[]{:S(2)}) copy-start(s32[160,8]{0,1:T(8,128)} %param.12) | copy-start | bytes 15364
  74.0 5.9 %copy-start.1 = (f32[160,8]{0,1:T(8,128)S(1)}, f32[160,8]{0,1:T(8,128)}, u32[]{:S(2)}) copy-start(f32[160,8]{0,1:T(8,128)} %param.13) | copy-start | bytes 15364
  74.0 49.8 %all-to-all-start.1 = ((bf16[2,4,5,32,1536]{4,3,1,2,0:T(8,128)(2,1)}), bf16[2,4,5,32,1536]{4,3,1,2,0:T(8,128)(2,1)}, u32[]{:S(2)}, u32[]{:S(2)}) async-start(bf16[2,4,5,32,1536]{4,3,1,2,0:T(8,128)(2,1)} %copy.21), calls=%async_computation.1 | async-start | bytes 7864320 | tf_op jit(solution)/shard_map/all_to_all | solution.py:31
where the time goes:
time: 146 us; the launch traced here: 145 us
  blocking collectives  49.7 us (34%)
  waiting for transfers between devices  43.6 us (30%)
  local copies, waits for them, and re-layouts  21.3 us (15%)
  matrix products  19.4 us (13%)
  other arithmetic  5.7 us (4%)
  starting transfers between devices  5.64 us (4%)
    all_to_all x1, blocking collectives, local_step(): y_inner = lax.all_to_all(y_split, 'expert', 1, 1, tiled=True)  49.7 us
    all_to_all x1, waiting for transfers between devices, local_step(): y_recv = lax.all_to_all(y_inner, 'outer', 0, 0, tiled=True)  43.6 us
    dot_general x1, matrix products, expert_rows(): jnp.einsum('secf,efd->secd', hidden, w_down, preferred_element_type=jnp.f...  12.9 us
    gather x1, local copies, waits for them, and re-layouts, weighted_sum(): picked = jnp.take(y_flat, flat_idx, axis=0)  11.5 us
    dot_general x1, matrix products, expert_rows(): jnp.einsum('secd,edf->secf', x_disp, w_up, preferred_element_type=jnp.flo...  6.53 us
    reduce_sum x1, other arithmetic, weighted_sum(): jnp.sum(picked.astype(jnp.float32) * weight[:, :, None], axis=1)  5.68 us
    all_to_all x1, starting transfers between devices, local_step(): y_recv = lax.all_to_all(y_inner, 'outer', 0, 0, tiled=True)  5.64 us
    all_to_all x1, local copies, waits for them, and re-layouts, local_step(): y_recv = lax.all_to_all(y_inner, 'outer', 0, 0, tiled=True)  4.45 us
  transfers between devices with their start and end apart: 1, of which 1 were waited for; matrix products, arithmetic and copies ran while one was open for 0% of the time, Pallas kernels for 0%

commit v1 on v0

v1 whole, which is shorter than its diff:
```python
import functools

import jax
import jax.numpy as jnp
from jax import lax
from jax.experimental import pallas as pl
from jax.experimental.pallas import tpu as pltpu
from jax.sharding import PartitionSpec as P

XW = 640
GROUPS = ((640, 384), (1024, 256), (1280, 256))
BF16_MAX = 3.3895313892515355e38


def kernel(x_hbm, wg_hbm, wu_hbm, wd_hbm, slot_ref, ids_ref, gate_ref, out_ref,
           x_v, wg_v, wu_v, wd_v, h_v, y_send, r_x, r_y, tok, tok_r, st_f32,
           s_mat, used, z_send, z_recv, w_send, w_recv, acc,
           in_sems, tok_ssem, tok_rsem, x_ssem, x_rsem, y_ssem, y_rsem,
           z_ssem, z_rsem, w_ssem, w_rsem):
    b = lax.axis_index("outer")
    q = lax.axis_index("expert")
    x = q // 2
    c = q % 2
    experts = x_v.shape[0]
    cap = x_v.shape[2]
    blk = experts * cap
    toks = out_ref.shape[0]

    def dev(bb, xx, cc):
        return {"outer": bb, "expert": 2 * xx + cc}

    row = [(b, x, c), (b, x, 1 - c), (b, 1 - x, c), (b, 1 - x, 1 - c)]
    col = [(b, x, c), (b, x, 1 - c), (1 - b, x, c), (1 - b, x, 1 - c)]
    x_partner = dev(b, 1 - x, c)
    y_partner = dev(1 - b, x, c)

    def in_copies(e):
        return (pltpu.make_async_copy(x_hbm.at[:, e], x_v.at[e], in_sems.at[0, e]),
                pltpu.make_async_copy(wg_hbm.at[e], wg_v.at[e], in_sems.at[1, e]),
                pltpu.make_async_copy(wu_hbm.at[e], wu_v.at[e], in_sems.at[2, e]),
                pltpu.make_async_copy(wd_hbm.at[e], wd_v.at[e], in_sems.at[3, e]))

    def remote(src, dst, ssem, rsem, device):
        return pltpu.make_async_remote_copy(
            src_ref=src, dst_ref=dst, send_sem=ssem, recv_sem=rsem,
            device_id=device, device_id_type=pl.DeviceIdType.MESH)

    def x_copy(k, e):
        _, xx, cc = row[k]
        return remote(y_send.at[e, :, xx, cc, :, pl.ds(0, XW)], r_x.at[:, k, e],
                      x_ssem.at[k, e], x_rsem.at[k, e], dev(*row[k]))

    def y_copy(g, k, e):
        bb, _, cc = col[k]
        start, width = GROUPS[g]
        return remote(y_send.at[e, bb, :, cc, :, pl.ds(start, width)],
                      r_y.at[:, k, e, :, pl.ds(start - XW, width)],
                      y_ssem.at[g, k, e], y_rsem.at[g, k, e], dev(*col[k]))

    def z_copy(g):
        start, width = GROUPS[g]
        cols = pl.ds(start - XW, width)
        return remote(z_send.at[:, cols], z_recv.at[:, cols], z_ssem.at[g], z_rsem.at[g], x_partner)

    w_copy = remote(w_send, w_recv, w_ssem, w_rsem, y_partner)
    tok_copies = [remote(tok, tok_r.at[0], tok_ssem.at[0], tok_rsem.at[0], x_partner),
                  remote(tok, tok_r.at[1], tok_ssem.at[1], tok_rsem.at[1], y_partner)]

    for e in range(2):
        for cp in in_copies(e):
            cp.start()

    barrier = pltpu.get_barrier_semaphore()
    for peer in (row[1], row[2], row[3], col[2], col[3]):
        pl.semaphore_signal(barrier, inc=1, device_id=dev(*peer), device_id_type=pl.DeviceIdType.MESH)

    slot = slot_ref[...]
    flat = jnp.where(slot >= 0, ids_ref[...] * cap + slot, -1).astype(jnp.float32)
    tok[...] = jnp.full(tok.shape, -1.0, jnp.float32)
    tok[0:8, 0:toks] = flat
    tok[8:16, 0:toks] = gate_ref[...]

    pl.semaphore_wait(barrier, 5)
    for cp in tok_copies:
        cp.start()

    def ffn(e, carry):
        for cp in in_copies(e):
            cp.wait()

        @pl.when(e + 2 < experts)
        def _():
            for cp in in_copies(e + 2):
                cp.start()

        xs = x_v[e].reshape(8 * cap, x_v.shape[3])
        ff = h_v.shape[1]
        for n in range(0, ff, 256):
            g = jnp.dot(xs, wg_v[e, :, n:n + 256], preferred_element_type=jnp.float32)
            u = jnp.dot(xs, wu_v[e, :, n:n + 256], preferred_element_type=jnp.float32)
            h_v[:, n:n + 256] = (jax.nn.silu(g) * u).astype(jnp.bfloat16)
        h = h_v[...]
        for n in range(0, y_send.shape[5], 256):
            y = jnp.dot(h, wd_v[e, :, n:n + 256], preferred_element_type=jnp.float32)
            y_send[e, :, :, :, :, n:n + 256] = y.astype(jnp.bfloat16).reshape(2, 2, 2, cap, 256)
        r_x[:, 0, e] = y_send[e, :, x, c, :, 0:XW]
        r_y[:, 0, e] = y_send[e, b, :, c, :, XW:]
        for k in (2, 3, 1):
            x_copy(k, e).start()
            y_copy(0, k, e).start()
        return carry

    lax.fori_loop(0, experts, ffn, 0)

    for g in range(1, len(GROUPS)):
        for e in range(experts):
            for k in (2, 3, 1):
                y_copy(g, k, e).start()

    def build(i, tok_val, devices):
        rows = lax.broadcasted_iota(jnp.int32, (blk, tok_val.shape[1]), 0)
        for k in range(4):
            bb, xx, cc = devices[k]
            want = (rows + blk * (4 * bb + 2 * xx + cc)).astype(jnp.float32)
            s = jnp.zeros(want.shape, jnp.float32)
            for j in range(8):
                s = s + jnp.where(tok_val[j:j + 1, :] == want, tok_val[8 + j:9 + j, :], 0.0)
            st_f32[k * blk:(k + 1) * blk, :] = s
            hit = jnp.max(s, axis=1, keepdims=True)
            used[i, k * blk:(k + 1) * blk, :] = jnp.broadcast_to(
                jnp.where(hit > 0.0, 1.0, 0.0), (blk, 128)).astype(jnp.bfloat16)
        for m in range(0, 4 * blk, 128):
            t = jnp.transpose(st_f32[m:m + 128, :])[0:toks, :]
            s1 = jnp.minimum(t, BF16_MAX).astype(jnp.bfloat16)
            t = t - s1.astype(jnp.float32)
            s2 = t.astype(jnp.bfloat16)
            s3 = (t - s2.astype(jnp.float32)).astype(jnp.bfloat16)
            s_mat[i, 0:toks, m:m + 128] = s1
            s_mat[i, toks:2 * toks, m:m + 128] = s2
            s_mat[i, 2 * toks:3 * toks, m:m + 128] = s3

    def combine(i, rows, start, write):
        width = rows.shape[4]
        for n in range(0, width, 128):
            r = rows[:, :, :, :, n:n + 128].reshape(4 * blk, 128)
            r = jnp.where(used[i] > 0, r, jnp.zeros_like(r))
            o = jnp.dot(s_mat[i], r, preferred_element_type=jnp.float32)
            write(start + n, o[0:toks] + o[toks:2 * toks] + o[2 * toks:3 * toks])

    for cp in tok_copies:
        cp.wait_recv()
    build(0, tok_r[0], col)
    build(1, tok[...], col)
    build(2, tok_r[1], row)
    build(3, tok[...], row)

    def put_z(n, v):
        z_send[:, n:n + 128] = v

    def put_w(n, v):
        w_send[:, n:n + 128] = v.astype(jnp.bfloat16)

    def put_acc(n, v):
        acc[:, n:n + 128] = v

    def y_group(g):
        start, width = GROUPS[g]
        cols = pl.ds(start - XW, width)
        for e in range(experts):
            for k in (1, 2, 3):
                y_copy(g, k, e).wait_recv()
        combine(0, r_y.at[pl.ds(1 - x, 1), :, :, :, cols], start - XW, put_z)
        z_copy(g).start()
        combine(1, r_y.at[pl.ds(x, 1), :, :, :, cols], start, put_acc)

    y_group(0)
    y_group(1)
    for e in range(experts):
        for k in (1, 2, 3):
            x_copy(k, e).wait_recv()
    combine(2, r_x.at[pl.ds(1 - b, 1)], 0, put_w)
    w_copy.start()
    combine(3, r_x.at[pl.ds(b, 1)], 0, put_acc)
    y_group(2)

    for g, (start, width) in enumerate(GROUPS):
        z_copy(g).wait_recv()
        out_ref[:, start:start + width] = (
            acc[:, start:start + width] + z_recv[:, start - XW:start - XW + width]).astype(jnp.bfloat16)
    w_copy.wait_recv()
    out_ref[:, 0:XW] = (acc[:, 0:XW] + w_recv[...].astype(jnp.float32)).astype(jnp.bfloat16)

    for cp in tok_copies:
        cp.wait_send()
    for e in range(experts):
        for k in (1, 2, 3):
            x_copy(k, e).wait_send()
            for g in range(len(GROUPS)):
                y_copy(g, k, e).wait_send()
    for g in range(len(GROUPS)):
        z_copy(g).wait_send()
    w_copy.wait_send()


def solution(mesh):
    def local_step(x_disp, w_gate, w_up, w_down, slot_idx, expert_ids, gate_wts):
        sources, experts, cap, width = x_disp.shape
        ff = w_gate.shape[2]
        toks = slot_idx.shape[0]
        yw = width - XW
        ng = len(GROUPS)
        dma = pltpu.SemaphoreType.DMA
        bf16, f32 = jnp.bfloat16, jnp.float32
        vmem = pl.BlockSpec(memory_space=pltpu.VMEM)
        hbm = pl.BlockSpec(memory_space=pl.ANY)
        rows = 4 * experts * cap
        return pl.pallas_call(
            kernel,
            out_shape=jax.ShapeDtypeStruct((toks, width), bf16),
            in_specs=[hbm] * 4 + [vmem] * 3,
            out_specs=vmem,
            scratch_shapes=[
                pltpu.VMEM((experts, sources, cap, width), bf16),
                pltpu.VMEM((experts, width, ff), bf16),
                pltpu.VMEM((experts, width, ff), bf16),
                pltpu.VMEM((experts, ff, width), bf16),
                pltpu.VMEM((sources * cap, ff), bf16),
                pltpu.VMEM((experts, 2, 2, 2, cap, width), bf16),
                pltpu.VMEM((2, 4, experts, cap, XW), bf16),
                pltpu.VMEM((2, 4, experts, cap, yw), bf16),
                pltpu.VMEM((16, 256), f32),
                pltpu.VMEM((2, 16, 256), f32),
                pltpu.VMEM((rows, 256), f32),
                pltpu.VMEM((4, 3 * toks, rows), bf16),
                pltpu.VMEM((4, rows, 128), bf16),
                pltpu.VMEM((toks, yw), f32),
                pltpu.VMEM((toks, yw), f32),
                pltpu.VMEM((toks, XW), bf16),
                pltpu.VMEM((toks, XW), bf16),
                pltpu.VMEM((toks, width), f32),
                dma((4, experts)), dma((2,)), dma((2,)),
                dma((4, experts)), dma((4, experts)),
                dma((ng, 4, experts)), dma((ng, 4, experts)),
                dma((ng,)), dma((ng,)), dma, dma,
            ],
            compiler_params=pltpu.CompilerParams(
                collective_id=0, has_side_effects=True, vmem_limit_bytes=60 * 2**20),
            name="moe",
        )(x_disp, w_gate, w_up, w_down, slot_idx.T, expert_ids.T, gate_wts.T)

    expert_spec = P(("outer", "expert"))
    token_spec = P(("data", "outer", "expert"))
    return jax.shard_map(local_step, mesh=mesh, in_specs=(P("data", ("outer", "expert")), expert_spec, expert_spec, expert_spec, token_spec, token_spec, token_spec), out_specs=token_spec, check_vma=False)
```

time: 146 us -> 44.7 us (0.31)
  blocking collectives: 49.7 us -> 0 us
  waiting for transfers between devices: 43.6 us -> 0 us
  Pallas kernels: 0 us -> 42.7 us
  local copies, waits for them, and re-layouts: 21.3 us -> 1.84 us
  matrix products: 19.4 us -> 0 us
  other arithmetic: 5.7 us -> 0 us
  starting transfers between devices: 5.64 us -> 0 us
    all_to_all x1 -> x0, blocking collectives: 49.7 us -> none  [local_step(): y_inner = lax.all_to_all(y_split, 'expert', 1, 1, tiled=True)]
    all_to_all x1 -> x0, waiting for transfers between devices: 43.6 us -> none  [local_step(): y_recv = lax.all_to_all(y_inner, 'outer', 0, 0, tiled=True)]
    pallas_call x0 -> x1, Pallas kernels: none -> 42.7 us  [local_step(): pl.pallas_call(kernel, out_shape=jax.ShapeDtypeStruct((toks, width), bf16...]
    dot_general x2 -> x0, matrix products: 19.4 us -> none  [the longest x1 12.9 us: expert_rows(): jnp.einsum('secf,efd->secd', hidden, w_down, preferred_element_type=jnp.f...]
    gather x1 -> x0, local copies, waits for them, and re-layouts: 11.5 us -> none  [weighted_sum(): picked = jnp.take(y_flat, flat_idx, axis=0)]
    all_to_all x2 -> x0, local copies, waits for them, and re-layouts: 6.78 us -> none  [the longest x1 4.45 us: local_step(): y_recv = lax.all_to_all(y_inner, 'outer', 0, 0, tiled=True)]
    reduce_sum x1 -> x0, other arithmetic: 5.68 us -> none  [weighted_sum(): jnp.sum(picked.astype(jnp.float32) * weight[:, :, None], axis=1)]
    all_to_all x1 -> x0, starting transfers between devices: 5.64 us -> none  [local_step(): y_recv = lax.all_to_all(y_inner, 'outer', 0, 0, tiled=True)]
  transfers between devices with their start and end apart: 1 -> 0, of which waited for: 1 -> 0; matrix products, arithmetic and copies ran while one was open for 0% -> 0% of each run, Pallas kernels for 0% -> 0%
where the time goes in v1:
time: 44.7 us; the launch traced here: 44.5 us
  Pallas kernels  42.7 us (96%)
  local copies, waits for them, and re-layouts  1.84 us (4%)
    pallas_call x1, Pallas kernels, local_step(): pl.pallas_call(kernel, out_shape=jax.ShapeDtypeStruct((toks, width), bf16...  42.7 us
    unnamed x1, local copies, waits for them, and re-layouts  1.84 us

profile of v1, /device:TPU:0, one launch (start us, length us, event | category | flops | bytes accessed | tf_op | source)
XLA Modules:
  0.0 44.5 jit_solution(11325992350693426133)
XLA Ops:
  0.0 42.7 %moe.1 = bf16[160,1536]{1,0:T(8,128)(2,1)} custom-call(bf16[8,5,32,1536]{3,2,1,0:T(8,128)(2,1)} %x_hbm.1, bf16[5,1536,512]{2,1,0:T(8,128)(2,1)} %wg_hbm.1, bf16[5,1536,512]{2,1,0:T(8,128)(2,1)} %wu_hbm.1, bf16[5,512,1536]{2,1,0:T(8,128)(2,1)} %wd_hbm.1, s32[8,160]{1,0:T(8,128)} %bitcast.3, s32[8,160]{1,0:T(8,128)} %bitcast.4, f32[8,160]{1,0:T(8,128)} %bitcast.5), custom_call_target="tpu_custom_call" | custom-call | tf_op jit(solution)/shard_map/moe/pallas_call | solution.py:217
  42.7 1.8 %copy.9 = bf16[160,1536]{1,0:T(8,128)(2,1)} copy(bf16[160,1536]{1,0:T(8,128)(2,1)} %moe.1) | data formatting | bytes 983040

commit v2 on v1

v2 whole, which is shorter than its diff:
```python
import functools

import jax
import jax.numpy as jnp
from jax import lax
from jax.experimental import pallas as pl
from jax.experimental.pallas import tpu as pltpu
from jax.sharding import PartitionSpec as P

XW = 640
GROUPS = ((640, 384), (1024, 256), (1280, 128), (1408, 128))
TILE = 256
BF16_MAX = 3.3895313892515355e38


def kernel(x_hbm, wg_hbm, wu_hbm, wd_hbm, slot_hbm, ids_hbm, gate_hbm, out_ref,
           slot_ref, ids_ref, gate_ref, x_v, wg_v, wu_v, wd_v, h_v, y_send, r_x, r_y, tok, tok_r, st_f32,
           s_mat, used, z_send, z_recv, w_send, w_recv, acc,
           in_sems, half_sems, map_sems, tok_ssem, tok_rsem, x_ssem, x_rsem, y_ssem, y_rsem,
           z_ssem, z_rsem, w_ssem, w_rsem):
    b = lax.axis_index("outer")
    q = lax.axis_index("expert")
    x = q // 2
    c = q % 2
    experts = x_v.shape[0]
    cap = x_v.shape[2]
    blk = experts * cap
    toks = out_ref.shape[0]

    def dev(bb, xx, cc):
        return {"outer": bb, "expert": 2 * xx + cc}

    row = [(b, x, c), (b, x, 1 - c), (b, 1 - x, c), (b, 1 - x, 1 - c)]
    col = [(b, x, c), (b, x, 1 - c), (1 - b, x, c), (1 - b, x, 1 - c)]
    x_partner = dev(b, 1 - x, c)
    y_partner = dev(1 - b, x, c)

    def rows_in(e):
        return pltpu.make_async_copy(x_hbm.at[:, e], x_v.at[e], in_sems.at[0, e % 2])

    def down_in(e):
        return pltpu.make_async_copy(wd_hbm.at[e], wd_v.at[e], in_sems.at[3, e % 2])

    def in_copies(e):
        return (rows_in(e),
                pltpu.make_async_copy(wg_hbm.at[e], wg_v.at[e], in_sems.at[1, e % 2]),
                pltpu.make_async_copy(wu_hbm.at[e], wu_v.at[e], in_sems.at[2, e % 2]),
                down_in(e))

    def remote(src, dst, ssem, rsem, device):
        return pltpu.make_async_remote_copy(
            src_ref=src, dst_ref=dst, send_sem=ssem, recv_sem=rsem,
            device_id=device, device_id_type=pl.DeviceIdType.MESH)

    def drain(ref, sem):
        pltpu.make_async_copy(ref, ref, sem).wait()

    others = pl.ds(1, 3)

    def x_copy(k, e):
        _, xx, cc = row[k]
        return remote(y_send.at[e, :, xx, cc, :, pl.ds(0, XW)], r_x.at[:, k, e],
                      x_ssem, x_rsem, dev(*row[k]))

    def y_copy(g, k, e):
        bb, _, cc = col[k]
        start, width = GROUPS[g]
        return remote(y_send.at[e, bb, :, cc, :, pl.ds(start, width)],
                      r_y.at[:, k, e, :, pl.ds(start - XW, width)],
                      y_ssem, y_rsem.at[g], dev(*col[k]))

    def z_copy(g):
        start, width = GROUPS[g]
        cols = pl.ds(start - XW, width)
        return remote(z_send.at[:, cols], z_recv.at[:, cols], z_ssem, z_rsem.at[g], x_partner)

    w_copy = remote(w_send, w_recv, w_ssem, w_rsem, y_partner)
    tok_copies = [remote(tok, tok_r.at[0], tok_ssem, tok_rsem.at[0], x_partner),
                  remote(tok, tok_r.at[1], tok_ssem, tok_rsem.at[1], y_partner)]

    def half_copies(n):
        cols = pl.ds(n * TILE, TILE)
        return (pltpu.make_async_copy(wg_hbm.at[0, :, cols], wg_v.at[0, :, cols], half_sems.at[0, n]),
                pltpu.make_async_copy(wu_hbm.at[0, :, cols], wu_v.at[0, :, cols], half_sems.at[1, n]))

    halves = wg_v.shape[2] // TILE
    map_copies = [pltpu.make_async_copy(src, dst, map_sems.at[i]) for i, (src, dst) in enumerate(
        ((slot_hbm, slot_ref), (ids_hbm, ids_ref), (gate_hbm, gate_ref)))]
    rows_in(0).start()
    for n in range(halves):
        for cp in half_copies(n):
            cp.start()
    down_in(0).start()
    for cp in map_copies:
        cp.start()

    barrier = pltpu.get_barrier_semaphore()
    for peer in (row[1], row[2], row[3], col[2], col[3]):
        pl.semaphore_signal(barrier, inc=1, device_id=dev(*peer), device_id_type=pl.DeviceIdType.MESH)

    def load_maps():
        for cp in map_copies:
            cp.wait()
        slot = slot_ref[...]
        flat = jnp.where(slot >= 0, ids_ref[...] * cap + slot, -1).astype(jnp.float32)
        tok[...] = jnp.full(tok.shape, -1.0, jnp.float32)
        tok[0:8, 0:toks] = flat
        tok[8:16, 0:toks] = gate_ref[...]

    def start_in(e):
        for cp in in_copies(e):
            cp.start()

    def up(e, n):
        xs = x_v[e].reshape(8 * cap, x_v.shape[3])
        g = jnp.dot(xs, wg_v[e, :, n:n + TILE], preferred_element_type=jnp.float32)
        u = jnp.dot(xs, wu_v[e, :, n:n + TILE], preferred_element_type=jnp.float32)
        h_v[:, n:n + TILE] = (jax.nn.silu(g) * u).astype(jnp.bfloat16)

    def down_and_send(e):
        h = h_v[...]
        sent = 0
        for n in range(0, y_send.shape[5], TILE):
            y = jnp.dot(h, wd_v[e, :, n:n + TILE], preferred_element_type=jnp.float32)
            y_send[e, :, :, :, :, n:n + TILE] = y.astype(jnp.bfloat16).reshape(2, 2, 2, cap, TILE)
            if sent == 0 and n + TILE >= XW:
                for k in (2, 3, 1):
                    x_copy(k, e).start()
                sent = 1
            if sent == 1 and n + TILE >= GROUPS[0][0] + GROUPS[0][1]:
                for k in (2, 3, 1):
                    y_copy(0, k, e).start()
                sent = 2
        r_x[:, 0, e] = y_send[e, :, x, c, :, 0:XW]
        r_y[:, 0, e] = y_send[e, b, :, c, :, XW:]

    rows_in(0).wait()
    for n in range(halves):
        for cp in half_copies(n):
            cp.wait()
        if n == 0:
            start_in(1)
        up(0, n * TILE)
        if n == 0:
            load_maps()
    with jax.named_scope('barrier'):
        pl.semaphore_wait(barrier, 5)
    for cp in tok_copies:
        cp.start()
    down_in(0).wait()
    start_in(2)
    down_and_send(0)

    def ffn(e, carry):
        with jax.named_scope('in_wait'):
            for cp in in_copies(e):
                cp.wait()

        @pl.when(e + 2 < experts)
        def _():
            start_in(e + 2)

        for n in range(0, h_v.shape[1], TILE):
            up(e, n)
        down_and_send(e)
        return carry

    lax.fori_loop(1, experts, ffn, 0)

    for g in range(1, len(GROUPS)):
        for e in range(experts):
            for k in (2, 3, 1):
                y_copy(g, k, e).start()

    def build(i, tok_val, devices):
        rows = lax.broadcasted_iota(jnp.int32, (blk, tok_val.shape[1]), 0)
        for k in range(4):
            bb, xx, cc = devices[k]
            want = (rows + blk * (4 * bb + 2 * xx + cc)).astype(jnp.float32)
            s = jnp.zeros(want.shape, jnp.float32)
            for j in range(8):
                s = s + jnp.where(tok_val[j:j + 1, :] == want, tok_val[8 + j:9 + j, :], 0.0)
            st_f32[k * blk:(k + 1) * blk, :] = s
            hit = jnp.max(s, axis=1, keepdims=True)
            used[i, k * blk:(k + 1) * blk, :] = jnp.broadcast_to(
                jnp.where(hit > 0.0, 1.0, 0.0), (blk, 128)).astype(jnp.bfloat16)
        for m in range(0, 4 * blk, 128):
            t = jnp.transpose(st_f32[m:m + 128, :])[0:toks, :]
            s1 = jnp.minimum(t, BF16_MAX).astype(jnp.bfloat16)
            t = t - s1.astype(jnp.float32)
            s2 = t.astype(jnp.bfloat16)
            s3 = (t - s2.astype(jnp.float32)).astype(jnp.bfloat16)
            s_mat[i, 0:toks, m:m + 128] = s1
            s_mat[i, toks:2 * toks, m:m + 128] = s2
            s_mat[i, 2 * toks:3 * toks, m:m + 128] = s3

    def combine(i, rows, start, write):
        width = rows.shape[4]
        for n in range(0, width, 128):
            r = rows[:, :, :, :, n:n + 128].reshape(4 * blk, 128)
            r = jnp.where(used[i] > 0, r, jnp.zeros_like(r))
            o = jnp.dot(s_mat[i], r, preferred_element_type=jnp.float32)
            write(start + n, o[0:toks] + o[toks:2 * toks] + o[2 * toks:3 * toks])

    with jax.named_scope('build'):
        for cp in tok_copies:
            cp.wait_recv()
        build(0, tok_r[0], col)
        build(1, tok[...], col)
        build(2, tok_r[1], row)
        build(3, tok[...], row)

    def put_z(n, v):
        z_send[:, n:n + 128] = v

    def put_w(n, v):
        w_send[:, n:n + 128] = v.astype(jnp.bfloat16)

    def put_acc(n, v):
        acc[:, n:n + 128] = v

    def y_group(g):
        start, width = GROUPS[g]
        cols = pl.ds(start - XW, width)
        with jax.named_scope(f'y_wait{g}'):
            drain(r_y.at[:, others, :, :, cols], y_rsem.at[g])
        with jax.named_scope(f'y_comb{g}'):
            combine(0, r_y.at[pl.ds(1 - x, 1), :, :, :, cols], start - XW, put_z)
            z_copy(g).start()
        with jax.named_scope(f'y_own{g}'):
            combine(1, r_y.at[pl.ds(x, 1), :, :, :, cols], start, put_acc)

    y_group(0)
    y_group(1)
    with jax.named_scope('x_wait'):
        drain(r_x.at[:, others], x_rsem)
    combine(2, r_x.at[pl.ds(1 - b, 1)], 0, put_w)
    w_copy.start()
    combine(3, r_x.at[pl.ds(b, 1)], 0, put_acc)
    y_group(2)

    y_group(3)

    def finish(g):
        start, width = GROUPS[g]
        with jax.named_scope(f'z_wait{g}'):
            z_copy(g).wait_recv()
        out_ref[:, start:start + width] = (
            acc[:, start:start + width] + z_recv[:, start - XW:start - XW + width]).astype(jnp.bfloat16)

    finish(0)
    finish(1)
    finish(2)
    with jax.named_scope('w_wait'):
        w_copy.wait_recv()
    out_ref[:, 0:XW] = (acc[:, 0:XW] + w_recv[...].astype(jnp.float32)).astype(jnp.bfloat16)
    finish(3)

    drain(tok_r, tok_ssem)
    drain(r_x.at[:, others], x_ssem)
    drain(r_y.at[:, others], y_ssem)
    drain(z_send, z_ssem)
    w_copy.wait_send()


def solution(mesh):
    def local_step(x_disp, w_gate, w_up, w_down, slot_idx, expert_ids, gate_wts):
        sources, experts, cap, width = x_disp.shape
        ff = w_gate.shape[2]
        toks = slot_idx.shape[0]
        yw = width - XW
        ng = len(GROUPS)
        dma = pltpu.SemaphoreType.DMA
        bf16, f32 = jnp.bfloat16, jnp.float32
        vmem = pl.BlockSpec(memory_space=pltpu.VMEM)
        hbm = pl.BlockSpec(memory_space=pl.ANY)
        rows = 4 * experts * cap
        return pl.pallas_call(
            kernel,
            out_shape=pltpu.VMEM((toks, width), bf16),
            in_specs=[hbm] * 7,
            out_specs=vmem,
            scratch_shapes=[
                pltpu.VMEM((8, toks), jnp.int32),
                pltpu.VMEM((8, toks), jnp.int32),
                pltpu.VMEM((8, toks), f32),
                pltpu.VMEM((experts, sources, cap, width), bf16),
                pltpu.VMEM((experts, width, ff), bf16),
                pltpu.VMEM((experts, width, ff), bf16),
                pltpu.VMEM((experts, ff, width), bf16),
                pltpu.VMEM((sources * cap, ff), bf16),
                pltpu.VMEM((experts, 2, 2, 2, cap, width), bf16),
                pltpu.VMEM((2, 4, experts, cap, XW), bf16),
                pltpu.VMEM((2, 4, experts, cap, yw), bf16),
                pltpu.VMEM((16, 256), f32),
                pltpu.VMEM((2, 16, 256), f32),
                pltpu.VMEM((rows, 256), f32),
                pltpu.VMEM((4, 3 * toks, rows), bf16),
                pltpu.VMEM((4, rows, 128), bf16),
                pltpu.VMEM((toks, yw), f32),
                pltpu.VMEM((toks, yw), f32),
                pltpu.VMEM((toks, XW), bf16),
                pltpu.VMEM((toks, XW), bf16),
                pltpu.VMEM((toks, width), f32),
                dma((4, 2)), dma((2, ff // TILE)), dma((3,)), dma, dma((2,)),
                dma, dma, dma, dma((ng,)), dma, dma((ng,)), dma, dma,
            ],
            compiler_params=pltpu.CompilerParams(
                collective_id=0, has_side_effects=True, vmem_limit_bytes=60 * 2**20),
            name="moe",
        )(x_disp, w_gate, w_up, w_down, slot_idx.T, expert_ids.T, gate_wts.T)

    expert_spec = P(("outer", "expert"))
    token_spec = P(("data", "outer", "expert"))
    return jax.shard_map(local_step, mesh=mesh, in_specs=(P("data", ("outer", "expert")), expert_spec, expert_spec, expert_spec, token_spec, token_spec, token_spec), out_specs=token_spec, check_vma=False)
```

time: 44.7 us -> 38.8 us (0.87)
  Pallas kernels: 42.7 us -> 37.9 us
  local copies, waits for them, and re-layouts: 1.84 us -> 0.78 us
    pallas_call x1, Pallas kernels: 42.7 us -> 37.9 us  [local_step(): pl.pallas_call(kernel, out_shape=pltpu.VMEM((toks, width), bf16), in_spec...]
    unnamed x1, local copies, waits for them, and re-layouts: 1.84 us -> 0.78 us
where the time goes in v2:
time: 38.8 us; the launch traced here: 38.7 us
  Pallas kernels  37.9 us (98%)
  local copies, waits for them, and re-layouts  0.78 us (2%)
    pallas_call x1, Pallas kernels, local_step(): pl.pallas_call(kernel, out_shape=pltpu.VMEM((toks, width), bf16), in_spec...  37.9 us
    unnamed x1, local copies, waits for them, and re-layouts  0.78 us

profile of v2, /device:TPU:0, one launch (start us, length us, event | category | flops | bytes accessed | tf_op | source)
XLA Modules:
  0.0 38.7 jit_solution(3518962718021020010)
XLA Ops:
  0.0 37.9 %moe.1 = bf16[160,1536]{1,0:T(8,128)(2,1)S(1)} custom-call(bf16[8,5,32,1536]{3,2,1,0:T(8,128)(2,1)} %x_hbm.1, bf16[5,1536,512]{2,1,0:T(8,128)(2,1)} %wg_hbm.1, bf16[5,1536,512]{2,1,0:T(8,128)(2,1)} %wu_hbm.1, bf16[5,512,1536]{2,1,0:T(8,128)(2,1)} %wd_hbm.1, s32[8,160]{1,0:T(8,128)} %bitcast.3, s32[8,160]{1,0:T(8,128)} %bitcast.4, f32[8,160]{1,0:T(8,128)} %bitcast.5), custom_call_target="tpu_custom_call" | custom-call | tf_op jit(solution)/shard_map/moe/pallas_call | solution.py:278
  37.9 0.8 %copy.9 = bf16[160,1536]{1,0:T(8,128)(2,1)} copy(bf16[160,1536]{1,0:T(8,128)(2,1)S(1)} %moe.1) | data formatting | bytes 983040

commit v3 on v2

v3 whole, which is shorter than its diff:
```python
import functools

import jax
import jax.numpy as jnp
from jax import lax
from jax.experimental import pallas as pl
from jax.experimental.pallas import tpu as pltpu
from jax.sharding import PartitionSpec as P

XW = 640
TILE = 256
STEP = 512
K_STEP = 256
Z_LAST = 128
BF16_MAX = 3.3895313892515355e38


def kernel(x_hbm, wg_hbm, wu_hbm, wd_hbm, slot_hbm, ids_hbm, gate_hbm, out_ref,
           slot_ref, ids_ref, gate_ref, x_v, wg_v, wu_v, wd_v, g_v, u_v, h_v, y_send, r_x, r_y, tok, tok_r, st_f32,
           s_mat, used, z_send, z_recv, w_send, w_recv, acc,
           in_sems, first_sems, map_sems, tok_ssem, tok_rsem, x_ssem, x_rsem, y_ssem, y_rsem,
           z_ssem, z_rsem, w_ssem, w_rsem):
    b = lax.axis_index("outer")
    q = lax.axis_index("expert")
    x = q // 2
    c = q % 2
    experts = x_v.shape[0]
    cap = x_v.shape[2]
    blk = experts * cap
    toks, width = out_ref.shape

    def dev(bb, xx, cc):
        return {"outer": bb, "expert": 2 * xx + cc}

    row = [(b, x, c), (b, x, 1 - c), (b, 1 - x, c), (b, 1 - x, 1 - c)]
    col = [(b, x, c), (b, x, 1 - c), (1 - b, x, c), (1 - b, x, 1 - c)]
    x_partner = dev(b, 1 - x, c)
    y_partner = dev(1 - b, x, c)

    def rows_in(e):
        return pltpu.make_async_copy(x_hbm.at[:, e], x_v.at[e], in_sems.at[0, e % 2])

    def down_in(e):
        return pltpu.make_async_copy(wd_hbm.at[e], wd_v.at[e], in_sems.at[3, e % 2])

    def up_copies(e):
        return (rows_in(e),
                pltpu.make_async_copy(wg_hbm.at[e], wg_v.at[e], in_sems.at[1, e % 2]),
                pltpu.make_async_copy(wu_hbm.at[e], wu_v.at[e], in_sems.at[2, e % 2]))

    def start_in(e):
        for cp in up_copies(e):
            cp.start()
        down_in(e).start()

    def remote(src, dst, ssem, rsem, device):
        return pltpu.make_async_remote_copy(
            src_ref=src, dst_ref=dst, send_sem=ssem, recv_sem=rsem,
            device_id=device, device_id_type=pl.DeviceIdType.MESH)

    def drain(ref, sem):
        pltpu.make_async_copy(ref, ref, sem).wait()

    others = pl.ds(1, 3)

    def x_copy(k, e, start=0, stop=XW):
        _, xx, cc = row[k]
        cols = pl.ds(start, stop - start)
        return remote(y_send.at[e, :, xx, cc, :, cols], r_x.at[:, k, e, :, cols],
                      x_ssem, x_rsem, dev(*row[k]))

    def y_copy(own, k, e, start, stop):
        bb, _, cc = col[k]
        xx = x if own else 1 - x
        return remote(y_send.at[e, bb, xx, cc, :, pl.ds(start, stop - start)],
                      r_y.at[xx, k, e, :, pl.ds(start - XW, stop - start)],
                      y_ssem, y_rsem.at[own], dev(*col[k]))

    yw = z_send.shape[1]
    z_parts = [(0, yw - Z_LAST), (yw - Z_LAST, Z_LAST)]

    def z_copy(g):
        cols = pl.ds(*z_parts[g])
        return remote(z_send.at[:, cols], z_recv.at[:, cols], z_ssem, z_rsem.at[g], x_partner)

    w_copy = remote(w_send, w_recv, w_ssem, w_rsem, y_partner)
    tok_copies = [remote(tok, tok_r.at[0], tok_ssem, tok_rsem.at[0], x_partner),
                  remote(tok, tok_r.at[1], tok_ssem, tok_rsem.at[1], y_partner)]

    def first_up(m):
        ks = pl.ds(m * K_STEP, K_STEP)
        return (pltpu.make_async_copy(x_hbm.at[:, 0, :, ks], x_v.at[0, :, :, ks], first_sems.at[0, m]),
                pltpu.make_async_copy(wg_hbm.at[0, ks], wg_v.at[0, ks], first_sems.at[1, m]),
                pltpu.make_async_copy(wu_hbm.at[0, ks], wu_v.at[0, ks], first_sems.at[2, m]))

    def first_down(m):
        cols = pl.ds(m * STEP, STEP)
        return pltpu.make_async_copy(wd_hbm.at[0, :, cols], wd_v.at[0, :, cols], first_sems.at[3, m])

    steps = wg_v.shape[1] // K_STEP
    map_copies = [pltpu.make_async_copy(src, dst, map_sems.at[i]) for i, (src, dst) in enumerate(
        ((slot_hbm, slot_ref), (ids_hbm, ids_ref), (gate_hbm, gate_ref)))]
    for m in range(steps):
        for cp in first_up(m):
            cp.start()
    for m in range(width // STEP):
        first_down(m).start()
    for cp in map_copies:
        cp.start()
    start_in(1)

    barrier = pltpu.get_barrier_semaphore()
    for peer in (row[1], row[2], row[3], col[2], col[3]):
        pl.semaphore_signal(barrier, inc=1, device_id=dev(*peer), device_id_type=pl.DeviceIdType.MESH)

    def load_maps():
        for cp in map_copies:
            cp.wait()
        slot = slot_ref[...]
        flat = jnp.where(slot >= 0, ids_ref[...] * cap + slot, -1).astype(jnp.float32)
        tok[...] = jnp.full(tok.shape, -1.0, jnp.float32)
        tok[0:8, 0:toks] = flat
        tok[8:16, 0:toks] = gate_ref[...]


    def up(e, n):
        xs = x_v[e].reshape(8 * cap, x_v.shape[3])
        g = jnp.dot(xs, wg_v[e, :, n:n + TILE], preferred_element_type=jnp.float32)
        u = jnp.dot(xs, wu_v[e, :, n:n + TILE], preferred_element_type=jnp.float32)
        h_v[:, n:n + TILE] = (jax.nn.silu(g) * u).astype(jnp.bfloat16)

    def down(e, n):
        y = jnp.dot(h_v[...], wd_v[e, :, n:n + STEP], preferred_element_type=jnp.float32)
        y_send[e, :, :, :, :, n:n + STEP] = y.astype(jnp.bfloat16).reshape(2, 2, 2, cap, STEP)

    def keep_own(e):
        r_x[:, 0, e] = y_send[e, :, x, c, :, 0:XW]
        r_y[:, 0, e] = y_send[e, b, :, c, :, XW:]

    def send_x(e, start, stop):
        for k in (2, 3, 1):
            x_copy(k, e, start, stop).start()

    def send_y(own, e, start, stop):
        for k in (2, 3, 1):
            y_copy(own, k, e, start, stop).start()

    for m in range(steps):
        with jax.named_scope(f'f_wait{m}'):
            for cp in first_up(m):
                cp.wait()
        with jax.named_scope(f'f_up{m}'):
            ks = slice(m * K_STEP, (m + 1) * K_STEP)
            rows = x_v[0, :, :, ks].reshape(8 * cap, K_STEP)
            for n in range(0, h_v.shape[1], TILE):
                cols = slice(n, n + TILE)
                g = jnp.dot(rows, wg_v[0, ks, cols], preferred_element_type=jnp.float32)
                u = jnp.dot(rows, wu_v[0, ks, cols], preferred_element_type=jnp.float32)
                if m > 0:
                    g = g_v[:, cols] + g
                    u = u_v[:, cols] + u
                if m < steps - 1:
                    g_v[:, cols] = g
                    u_v[:, cols] = u
                else:
                    h_v[:, cols] = (jax.nn.silu(g) * u).astype(jnp.bfloat16)
    with jax.named_scope('down0'):
        first_down(0).wait()
        down(0, 0)
    with jax.named_scope('barrier'):
        pl.semaphore_wait(barrier, 5)
    send_x(0, 0, STEP)
    with jax.named_scope('down1'):
        first_down(1).wait()
        down(0, STEP)
        send_x(0, STEP, XW)
        send_y(0, 0, XW, 2 * STEP)
    with jax.named_scope('down2'):
        first_down(2).wait()
        start_in(2)
        down(0, 2 * STEP)
        send_y(0, 0, 2 * STEP, width)
    load_maps()
    keep_own(0)
    for cp in tok_copies:
        cp.start()

    def ffn(e, carry):
        with jax.named_scope('in_wait'):
            for cp in up_copies(e):
                cp.wait()
        for n in range(0, h_v.shape[1], TILE):
            up(e, n)
        with jax.named_scope('d_wait'):
            down_in(e).wait()

        @pl.when(e + 2 < experts)
        def _():
            start_in(e + 2)

        down(e, 0)
        send_x(e, 0, STEP)
        down(e, STEP)
        send_x(e, STEP, XW)
        send_y(0, e, XW, 2 * STEP)
        down(e, 2 * STEP)
        send_y(0, e, 2 * STEP, width)
        keep_own(e)
        return carry

    lax.fori_loop(1, experts, ffn, 0)

    for e in range(experts):
        send_y(1, e, XW, width)

    def build(i, tok_val, devices):
        rows = lax.broadcasted_iota(jnp.int32, (blk, tok_val.shape[1]), 0)
        for k in range(4):
            bb, xx, cc = devices[k]
            want = (rows + blk * (4 * bb + 2 * xx + cc)).astype(jnp.float32)
            s = jnp.zeros(want.shape, jnp.float32)
            for j in range(8):
                s = s + jnp.where(tok_val[j:j + 1, :] == want, tok_val[8 + j:9 + j, :], 0.0)
            st_f32[k * blk:(k + 1) * blk, :] = s
            hit = jnp.max(s, axis=1, keepdims=True)
            used[i, k * blk:(k + 1) * blk, :] = jnp.broadcast_to(
                jnp.where(hit > 0.0, 1.0, 0.0), (blk, 128)).astype(jnp.bfloat16)
        for m in range(0, 4 * blk, 128):
            t = jnp.transpose(st_f32[m:m + 128, :])[0:toks, :]
            s1 = jnp.minimum(t, BF16_MAX).astype(jnp.bfloat16)
            t = t - s1.astype(jnp.float32)
            s2 = t.astype(jnp.bfloat16)
            s3 = (t - s2.astype(jnp.float32)).astype(jnp.bfloat16)
            s_mat[i, 0:toks, m:m + 128] = s1
            s_mat[i, toks:2 * toks, m:m + 128] = s2
            s_mat[i, 2 * toks:3 * toks, m:m + 128] = s3

    def combine(i, rows, start, stop, write):
        for n in range(start, stop, 128):
            r = rows[:, :, :, n:n + 128].reshape(4 * blk, 128)
            r = jnp.where(used[i] > 0, r, jnp.zeros_like(r))
            o = jnp.dot(s_mat[i], r, preferred_element_type=jnp.float32)
            write(n, o[0:toks] + o[toks:2 * toks] + o[2 * toks:3 * toks])

    with jax.named_scope('build'):
        for cp in tok_copies:
            cp.wait_recv()
        build(0, tok_r[0], col)
        build(1, tok[...], col)
        build(2, tok_r[1], row)
        build(3, tok[...], row)

    def put_z(n, v):
        z_send[:, n:n + 128] = v

    def put_w(n, v):
        w_send[:, n:n + 128] = v.astype(jnp.bfloat16)

    def put_x(n, v):
        acc[:, n:n + 128] = v

    def put_y(n, v):
        acc[:, XW + n:XW + n + 128] = v

    with jax.named_scope('y_wait'):
        drain(r_y.at[1 - x, others], y_rsem.at[0])
    with jax.named_scope('y_comb'):
        for g, (start, size) in enumerate(z_parts):
            combine(0, r_y.at[1 - x], start, start + size, put_z)
            z_copy(g).start()
    with jax.named_scope('x_wait'):
        drain(r_x.at[:, others], x_rsem)
    with jax.named_scope('x_comb'):
        combine(2, r_x.at[1 - b], 0, XW, put_w)
        w_copy.start()
    with jax.named_scope('x_own'):
        combine(3, r_x.at[b], 0, XW, put_x)
    with jax.named_scope('o_wait'):
        drain(r_y.at[x, others], y_rsem.at[1])
    with jax.named_scope('y_own'):
        combine(1, r_y.at[x], 0, yw, put_y)

    def finish(g):
        start, size = z_parts[g]
        with jax.named_scope(f'z_wait{g}'):
            z_copy(g).wait_recv()
        out_ref[:, XW + start:XW + start + size] = (
            acc[:, XW + start:XW + start + size] + z_recv[:, start:start + size]).astype(jnp.bfloat16)

    for g in range(len(z_parts) - 1):
        finish(g)
    with jax.named_scope('w_wait'):
        w_copy.wait_recv()
    out_ref[:, 0:XW] = (acc[:, 0:XW] + w_recv[...].astype(jnp.float32)).astype(jnp.bfloat16)
    finish(len(z_parts) - 1)

    drain(tok_r, tok_ssem)
    drain(r_x.at[:, others], x_ssem)
    drain(r_y.at[:, others], y_ssem)
    drain(z_send, z_ssem)
    w_copy.wait_send()


def solution(mesh):
    def local_step(x_disp, w_gate, w_up, w_down, slot_idx, expert_ids, gate_wts):
        sources, experts, cap, width = x_disp.shape
        ff = w_gate.shape[2]
        toks = slot_idx.shape[0]
        yw = width - XW
        dma = pltpu.SemaphoreType.DMA
        bf16, f32 = jnp.bfloat16, jnp.float32
        vmem = pl.BlockSpec(memory_space=pltpu.VMEM)
        hbm = pl.BlockSpec(memory_space=pl.ANY)
        rows = 4 * experts * cap
        return pl.pallas_call(
            kernel,
            out_shape=pltpu.VMEM((toks, width), bf16),
            in_specs=[hbm] * 7,
            out_specs=vmem,
            scratch_shapes=[
                pltpu.VMEM((8, toks), jnp.int32),
                pltpu.VMEM((8, toks), jnp.int32),
                pltpu.VMEM((8, toks), f32),
                pltpu.VMEM((experts, sources, cap, width), bf16),
                pltpu.VMEM((experts, width, ff), bf16),
                pltpu.VMEM((experts, width, ff), bf16),
                pltpu.VMEM((experts, ff, width), bf16),
                pltpu.VMEM((sources * cap, ff), f32),
                pltpu.VMEM((sources * cap, ff), f32),
                pltpu.VMEM((sources * cap, ff), bf16),
                pltpu.VMEM((experts, 2, 2, 2, cap, width), bf16),
                pltpu.VMEM((2, 4, experts, cap, XW), bf16),
                pltpu.VMEM((2, 4, experts, cap, yw), bf16),
                pltpu.VMEM((16, 256), f32),
                pltpu.VMEM((2, 16, 256), f32),
                pltpu.VMEM((rows, 256), f32),
                pltpu.VMEM((4, 3 * toks, rows), bf16),
                pltpu.VMEM((4, rows, 128), bf16),
                pltpu.VMEM((toks, yw), f32),
                pltpu.VMEM((toks, yw), f32),
                pltpu.VMEM((toks, XW), bf16),
                pltpu.VMEM((toks, XW), bf16),
                pltpu.VMEM((toks, width), f32),
                dma((4, 2)), dma((4, width // K_STEP)), dma((3,)), dma, dma((2,)),
                dma, dma, dma, dma((2,)), dma, dma((2,)), dma, dma,
            ],
            compiler_params=pltpu.CompilerParams(
                collective_id=0, has_side_effects=True, vmem_limit_bytes=60 * 2**20),
            name="moe",
        )(x_disp, w_gate, w_up, w_down, slot_idx.T, expert_ids.T, gate_wts.T)

    expert_spec = P(("outer", "expert"))
    token_spec = P(("data", "outer", "expert"))
    return jax.shard_map(local_step, mesh=mesh, in_specs=(P("data", ("outer", "expert")), expert_spec, expert_spec, expert_spec, token_spec, token_spec, token_spec), out_specs=token_spec, check_vma=False)
```

time: 38.8 us -> 38.2 us (0.985)
  Pallas kernels: 37.9 us -> 37.4 us
    pallas_call x1, Pallas kernels: 37.9 us -> 37.4 us  [local_step(): pl.pallas_call(kernel, out_shape=pltpu.VMEM((toks, width), bf16), in_spec...]
where the time goes in v3:
time: 38.2 us
  Pallas kernels  37.4 us (98%)
  local copies, waits for them, and re-layouts  0.78 us (2%)
    pallas_call x1, Pallas kernels, local_step(): pl.pallas_call(kernel, out_shape=pltpu.VMEM((toks, width), bf16), in_spec...  37.4 us
    unnamed x1, local copies, waits for them, and re-layouts  0.78 us

profile of v3, /device:TPU:0, one launch (start us, length us, event | category | flops | bytes accessed | tf_op | source)
XLA Modules:
  0.0 38.2 jit_solution(15984775594769386233)
XLA Ops:
  0.0 37.4 %moe.1 = bf16[160,1536]{1,0:T(8,128)(2,1)S(1)} custom-call(bf16[8,5,32,1536]{3,2,1,0:T(8,128)(2,1)} %x_hbm.1, bf16[5,1536,512]{2,1,0:T(8,128)(2,1)} %wg_hbm.1, bf16[5,1536,512]{2,1,0:T(8,128)(2,1)} %wu_hbm.1, bf16[5,512,1536]{2,1,0:T(8,128)(2,1)} %wd_hbm.1, s32[8,160]{1,0:T(8,128)} %bitcast.3, s32[8,160]{1,0:T(8,128)} %bitcast.4, f32[8,160]{1,0:T(8,128)} %bitcast.5), custom_call_target="tpu_custom_call" | custom-call | tf_op jit(solution)/shard_map/moe/pallas_call | solution.py:315
  37.4 0.8 %copy.9 = bf16[160,1536]{1,0:T(8,128)(2,1)} copy(bf16[160,1536]{1,0:T(8,128)(2,1)S(1)} %moe.1) | data formatting | bytes 983040

commit v4 on v3

--- a/solution.py
+++ b/solution.py
@@ -93,8 +93,11 @@
                 pltpu.make_async_copy(wg_hbm.at[0, ks], wg_v.at[0, ks], first_sems.at[1, m]),
                 pltpu.make_async_copy(wu_hbm.at[0, ks], wu_v.at[0, ks], first_sems.at[2, m]))
 
+    edges = (0, 256, 768, 1280, 1536)
+    pieces = tuple(zip(edges[:-1], edges[1:]))
+
     def first_down(m):
-        cols = pl.ds(m * STEP, STEP)
+        cols = pl.ds(pieces[m][0], pieces[m][1] - pieces[m][0])
         return pltpu.make_async_copy(wd_hbm.at[0, :, cols], wd_v.at[0, :, cols], first_sems.at[3, m])
 
     steps = wg_v.shape[1] // K_STEP
@@ -103,7 +106,7 @@
     for m in range(steps):
         for cp in first_up(m):
             cp.start()
-    for m in range(width // STEP):
+    for m in range(len(pieces)):
         first_down(m).start()
     for cp in map_copies:
         cp.start()
@@ -129,9 +132,9 @@
         u = jnp.dot(xs, wu_v[e, :, n:n + TILE], preferred_element_type=jnp.float32)
         h_v[:, n:n + TILE] = (jax.nn.silu(g) * u).astype(jnp.bfloat16)
 
-    def down(e, n):
-        y = jnp.dot(h_v[...], wd_v[e, :, n:n + STEP], preferred_element_type=jnp.float32)
-        y_send[e, :, :, :, :, n:n + STEP] = y.astype(jnp.bfloat16).reshape(2, 2, 2, cap, STEP)
+    def down(e, start, stop):
+        y = jnp.dot(h_v[...], wd_v[e, :, start:stop], preferred_element_type=jnp.float32)
+        y_send[e, :, :, :, :, start:stop] = y.astype(jnp.bfloat16).reshape(2, 2, 2, cap, stop - start)
 
     def keep_own(e):
         r_x[:, 0, e] = y_send[e, :, x, c, :, 0:XW]
@@ -166,20 +169,23 @@
                     h_v[:, cols] = (jax.nn.silu(g) * u).astype(jnp.bfloat16)
     with jax.named_scope('down0'):
         first_down(0).wait()
-        down(0, 0)
+        half = h_v.shape[0] // 2
+        for i in range(2):
+            y = jnp.dot(h_v[i * half:(i + 1) * half], wd_v[0, :, 0:TILE], preferred_element_type=jnp.float32)
+            y_send[0, i, :, :, :, 0:TILE] = y.astype(jnp.bfloat16).reshape(2, 2, cap, TILE)
     with jax.named_scope('barrier'):
         pl.semaphore_wait(barrier, 5)
-    send_x(0, 0, STEP)
-    with jax.named_scope('down1'):
-        first_down(1).wait()
-        down(0, STEP)
-        send_x(0, STEP, XW)
-        send_y(0, 0, XW, 2 * STEP)
-    with jax.named_scope('down2'):
-        first_down(2).wait()
-        start_in(2)
-        down(0, 2 * STEP)
-        send_y(0, 0, 2 * STEP, width)
+    send_x(0, 0, TILE)
+    for m in range(1, len(pieces)):
+        start, stop = pieces[m]
+        first_down(m).wait()
+        if m == 3:
+            start_in(2)
+        with jax.named_scope(f'down{m}'):
+            down(0, start, stop)
+            if start < XW:
+                send_x(0, start, XW)
+            send_y(0, 0, max(start, XW), stop)
     load_maps()
     keep_own(0)
     for cp in tok_copies:
@@ -198,12 +204,12 @@
         def _():
             start_in(e + 2)
 
-        down(e, 0)
+        down(e, 0, STEP)
         send_x(e, 0, STEP)
-        down(e, STEP)
+        down(e, STEP, 2 * STEP)
         send_x(e, STEP, XW)
         send_y(0, e, XW, 2 * STEP)
-        down(e, 2 * STEP)
+        down(e, 2 * STEP, width)
         send_y(0, e, 2 * STEP, width)
         keep_own(e)
         return carry

time: 38.2 us -> 38.2 us (level)
  no operation moved by 1% of the time
where the time goes in v4:
time: 38.2 us; the launch traced here: 38.1 us
  Pallas kernels  37.3 us (98%)
  local copies, waits for them, and re-layouts  0.78 us (2%)
    pallas_call x1, Pallas kernels, local_step(): pl.pallas_call(kernel, out_shape=pltpu.VMEM((toks, width), bf16), in_spec...  37.3 us
    unnamed x1, local copies, waits for them, and re-layouts  0.78 us

profile of v4, /device:TPU:0, one launch (start us, length us, event | category | flops | bytes accessed | tf_op | source)
XLA Modules:
  0.0 38.1 jit_solution(8868215323474715066)
XLA Ops:
  0.0 37.3 %moe.1 = bf16[160,1536]{1,0:T(8,128)(2,1)S(1)} custom-call(bf16[8,5,32,1536]{3,2,1,0:T(8,128)(2,1)} %x_hbm.1, bf16[5,1536,512]{2,1,0:T(8,128)(2,1)} %wg_hbm.1, bf16[5,1536,512]{2,1,0:T(8,128)(2,1)} %wu_hbm.1, bf16[5,512,1536]{2,1,0:T(8,128)(2,1)} %wd_hbm.1, s32[8,160]{1,0:T(8,128)} %bitcast.3, s32[8,160]{1,0:T(8,128)} %bitcast.4, f32[8,160]{1,0:T(8,128)} %bitcast.5), custom_call_target="tpu_custom_call" | custom-call | tf_op jit(solution)/shard_map/moe/pallas_call | solution.py:321
  37.3 0.8 %copy.9 = bf16[160,1536]{1,0:T(8,128)(2,1)} copy(bf16[160,1536]{1,0:T(8,128)(2,1)S(1)} %moe.1) | data formatting | bytes 983040
